TPU v7x, 32 devices: a whole 2x2x4 slice. The times are simulated.
32 devices in a mesh: ep: 8 (over z, x), etp: 4 (over y, core).
Axes of the slice: x: 2, y: 2, z: 4, core: 2. Of those that a mesh axis runs over, the one named last changes fastest.
Arguments:
- tokens: bfloat16 [1024, 4096], P('ep', 'etp'), may hold values from -6 to 6
- expert_ids: int32 [1024, 8], P('ep'), may hold values from 0 to 15, all different within a row; in each aligned block of 128 rows (0 to 127, 128 to 255, ...) at most 96 rows name the same one
- gate_prob: float32 [1024, 8], P('ep'), may hold values from 0.05 to 1
- gate_weight: bfloat16 [16, 4096, 1536], P('ep', None, 'etp'), may hold values from -0.09375 to 0.09375
- up_weight: bfloat16 [16, 4096, 1536], P('ep', None, 'etp'), may hold values from -0.09375 to 0.09375
- down_weight: bfloat16 [16, 1536, 4096], P('ep', 'etp'), may hold values from -0.15625 to 0.15625
Outputs:
- mixed: bfloat16 [1024, 4096], P('ep', 'etp')
Inputs may be any that keep to these rules, and one draw needn't show every extreme that they name: `expert_ids`: each row names 8 different experts. Within each aligned block of 128 rows (one token group) no expert is named more than 96 times, and in every draw some expert is named exactly 96 times in some block.
All inputs are finite; a program needn't handle non-finite values.
Results may differ from a plain program's by a relative error of at most 0.012.
Values may be sent and summed in bfloat16 or wider, within the bound.
A program may use at most 128 MiB of HBM per device.

v0:
```python
from functools import partial
import jax
import jax.numpy as jnp
from jax import lax
from jax.sharding import PartitionSpec as P


def add_features(totals, portion, offset, w_gate, w_up):
    return (
        jnp.dot(portion, w_gate, preferred_element_type=jnp.float32),
        jnp.dot(portion, w_up, preferred_element_type=jnp.float32),
    )


def body(tokens, expert_ids, gate_prob, gate_weight, up_weight, down_weight):
    groups = lax.axis_size("ep")
    local_experts = gate_weight.shape[0]
    experts = local_experts * groups
    tok_rows = expert_ids.shape[0]
    fanout = expert_ids.shape[1]
    capacity = max(2, 3 * tok_rows * fanout // (2 * experts))
    flat_ids = expert_ids.reshape(-1)
    onehot = (flat_ids[:, None] == jnp.arange(experts, dtype=jnp.int32)[None, :]).astype(jnp.int32)
    position = jnp.sum((jnp.cumsum(onehot, axis=0) - onehot) * onehot, axis=1)
    slot_index = flat_ids * capacity + position
    owners = jnp.arange(tok_rows * fanout, dtype=jnp.int32) // fanout
    source = jnp.full((experts * capacity,), tok_rows, jnp.int32).at[slot_index].set(owners)
    padded = jnp.concatenate([tokens, jnp.zeros((1, tokens.shape[1]), tokens.dtype)], axis=0)
    outgoing = padded[source].reshape(groups, local_experts, capacity, tokens.shape[1])
    arrived = lax.all_to_all(outgoing, "ep", split_axis=0, concat_axis=2, tiled=True)
    partials = []
    for member in range(local_experts):
        expert_rows = arrived[0, member]
        starting = jnp.zeros((expert_rows.shape[0], gate_weight.shape[2]), jnp.float32)
        folder = partial(add_features, w_gate=gate_weight[member], w_up=up_weight[member])
        gate_sum, up_sum = folder(
            (starting, starting),
            lax.all_gather(expert_rows, "etp", axis=1, tiled=True),
            jnp.int32(0),
        )
        hidden = (jax.nn.silu(gate_sum) * up_sum).astype(jnp.bfloat16)
        partials.append(jnp.dot(hidden, down_weight[member], preferred_element_type=jnp.float32))
    partial_all = jnp.stack(partials).reshape(local_experts, groups, capacity, down_weight.shape[2])
    combine_scale = gate_prob.reshape(tok_rows, fanout, 1)
    summed = lax.psum_scatter(
        partial_all.astype(jnp.bfloat16), "etp", scatter_dimension=3, tiled=True
    ).astype(jnp.float32)
    returned = lax.all_to_all(
        summed.astype(jnp.bfloat16), "ep", split_axis=1, concat_axis=0, tiled=True
    ).astype(summed.dtype)
    picked = returned.reshape(experts * capacity, -1)[slot_index].reshape(tok_rows, fanout, -1)
    mixed = jnp.sum(picked * combine_scale, axis=1).astype(jnp.bfloat16)
    return mixed


def solution(mesh):
    in_specs = (
        P("ep", "etp"),
        P("ep", None),
        P("ep", None),
        P("ep", None, "etp"),
        P("ep", None, "etp"),
        P("ep", "etp", None),
    )
    out_specs = P("ep", "etp")
    return jax.shard_map(body, mesh=mesh, in_specs=in_specs, out_specs=out_specs, check_vma=False)
```

profile of v0, /device:TPU:0, one launch (start us, length us, event | category | flops | bytes accessed | tf_op | source)
XLA Modules:
  0.0 419.7 jit_solution(9803007199391855178)
XLA Ops:
  6.5 0.8 copy.19
  8.2 4.5 %reduce-window.6 = s32[16,8,128]{2,1,0:T(8,128)S(1)} reduce-window(s32[16,8,128]{2,1,0:T(8,128)S(1)} %fusion.46, s32[]{:T(128)} %constant.32.clone.1), window={size=1x1x128 pad=0_0x0_0x127_0}, to_apply=%region_0.0 | reduce-window | flops 2080768 | bytes 131076 | tf_op jit(solution)/shard_map/reduce-window
  13.4 4.3 %scatter_custom_fusion = s32[1536]{0:T(1024)S(1)} fusion(s32[1024]{0:T(1024)S(1)} %bitcast.98, s32[1024]{0:T(1024)S(1)} %add_select_fusion, s32[]{:T(128)} %constant.30.clone.1), kind=kCustom, calls=%fused_computation.52 | custom fusion | bytes 6148 | tf_op jit(solution)/shard_map/scatter | solution.py:27
  17.7 1.0 concatenate.5
  18.7 5.1 %gather_fusion = bf16[1536,1024]{1,0:T(8,128)(2,1)S(1)} fusion(bf16[129,1024]{1,0:T(8,128)(2,1)S(1)} %concatenate.5, s32[2048]{0:T(1024)S(1)} %pad_clamp_fusion), kind=kCustom, calls=%fused_computation | custom fusion | bytes 6297600 | tf_op jit(solution)/shard_map/gather | solution.py:29
  23.8 77.8 %all_to_all.27 = bf16[8,2,96,1024]{3,2,1,0:T(8,128)(2,1)S(1)} all-to-all(bf16[8,2,96,1024]{3,2,1,0:T(8,128)(2,1)S(1)} %bitcast.92), channel_id=1, replica_groups=mesh['ep'=8,'etp'=4] {'ep'}, dimensions={0} | all-to-all | bytes 6291456 | tf_op jit(solution)/shard_map/all_to_all | solution.py:30
  102.0 1.9 fusion.52
  104.0 0.7 all-gather.7.cloned.1.call-update
  105.0 44.6 %all-gather.5.cloned.1.call-done = bf16[1,1,768,4096]{3,2,1,0:T(8,128)(2,1)} async-done(((bf16[1,1,768,1024]{3,2,1,0:T(8,128)(2,1)}), bf16[1,1,768,4096]{3,2,1,0:T(8,128)(2,1)}) %all-gather.5.cloned.1.call-update) | async-done | bytes 6291472 | tf_op jit(solution)/shard_map/all_gather | solution.py:38
  149.5 6.6 %fusion.6 = f32[768,384]{1,0:T(8,128)S(1)} fusion(bf16[1,1,768,4096]{3,2,1,0:T(8,128)(2,1)} %all-gather.5.cloned.1.call-done, bf16[2,4096,384]{2,1,0:T(8,128)(2,1)} %param.9), kind=kOutput, calls=%fused_computation.12 | convolution fusion | flops 2415919104 | bytes 10616832 | tf_op jit(solution)/shard_map/dot_general | solution.py:10
  156.1 5.9 %fusion.38 = bf16[768,384]{1,0:T(8,128)(2,1)S(1)} fusion(bf16[2,4096,384]{2,1,0:T(8,128)(2,1)} %param.10, bf16[1,1,768,4096]{3,2,1,0:T(8,128)(2,1)S(1)} %copy-done.1, f32[768,384]{1,0:T(8,128)S(1)} %fusion.6), kind=kOutput, calls=%fused_computation.34 | convolution fusion | flops 2417688576 | bytes 11206656 | tf_op jit(solution)/shard_map/dot_general | solution.py:11
  162.0 5.4 %fusion.8 = bf16[1,8,96,4096]{3,2,1,0:T(8,128)(2,1)} fusion(bf16[8,96,384]{2,1,0:T(8,128)(2,1)S(1)} %bitcast.104, bf16[2,384,4096]{2,1,0:T(8,128)(2,1)S(1)} %bitcast.101), kind=kOutput, calls=%fused_computation.14 | convolution fusion | flops 2419064832 | bytes 10027008 | tf_op jit(solution)/shard_map/dot_general | solution.py:42
  167.4 30.1 %all-gather.7.cloned.1.call-done = bf16[1,1,768,4096]{3,2,1,0:T(8,128)(2,1)} async-done(((bf16[1,1,768,1024]{3,2,1,0:T(8,128)(2,1)}), bf16[1,1,768,4096]{3,2,1,0:T(8,128)(2,1)}) %all-gather.7.cloned.1.call-update) | async-done | bytes 6291472 | tf_op jit(solution)/shard_map/all_gather | solution.py:38
  197.5 6.6 %fusion.2 = f32[768,384]{1,0:T(8,128)S(1)} fusion(bf16[1,1,768,4096]{3,2,1,0:T(8,128)(2,1)} %all-gather.7.cloned.1.call-done, bf16[2,4096,384]{2,1,0:T(8,128)(2,1)} %param.9), kind=kOutput, calls=%fused_computation.8 | convolution fusion | flops 2415919104 | bytes 10616832 | tf_op jit(solution)/shard_map/dot_general | solution.py:10
  204.1 5.7 %fusion.33 = bf16[768,384]{1,0:T(8,128)(2,1)S(1)} fusion(bf16[2,4096,384]{2,1,0:T(8,128)(2,1)} %param.10, bf16[1,1,768,4096]{3,2,1,0:T(8,128)(2,1)S(1)} %copy-done.2, f32[768,384]{1,0:T(8,128)S(1)} %fusion.2), kind=kOutput, calls=%fused_computation.33 | convolution fusion | flops 2417688576 | bytes 11206656 | tf_op jit(solution)/shard_map/dot_general | solution.py:11
  209.9 3.6 fusion.9
  213.5 5.3 %pad_maximum_fusion = bf16[2,8,96,4096]{3,2,1,0:T(8,128)(2,1)} fusion(bf16[1,8,96,4096]{3,2,1,0:T(8,128)(2,1)S(1)} %fusion.9, bf16[1,8,96,4096]{3,2,1,0:T(8,128)(2,1)S(1)} %bitcast.94), kind=kLoop, calls=%fused_computation.3 | loop fusion | flops 6291456 | bytes 25165824 | tf_op jit(solution)/shard_map/stack | solution.py:43
  218.8 97.3 %reduce-scatter.2.cloned.1.call-done = bf16[2,8,96,1024]{3,2,1,0:T(8,128)(2,1)} async-done(((bf16[2,8,96,4096]{3,2,1,0:T(8,128)(2,1)}), bf16[2,8,96,1024]{3,2,1,0:T(8,128)(2,1)}) %reduce-scatter.2.cloned.1.call-update) | async-done | bytes 3145744 | tf_op jit(solution)/shard_map/reduce_scatter | solution.py:45
  316.1 3.9 copy.24
  320.1 5.6 %all-to-all-start.1 = ((bf16[2,8,96,1024]{3,2,0,1:T(8,128)(2,1)}), bf16[2,8,96,1024]{3,2,0,1:T(8,128)(2,1)S(1)}, u32[]{:S(2)}, u32[]{:S(2)}) async-start(bf16[2,8,96,1024]{3,2,0,1:T(8,128)(2,1)} %copy.24), calls=%async_computation.2 | async-start | bytes 6291456 | tf_op jit(solution)/shard_map/all_to_all | solution.py:48
  325.8 70.4 %all-to-all-done.1 = bf16[2,8,96,1024]{3,2,0,1:T(8,128)(2,1)S(1)} async-done(((bf16[2,8,96,1024]{3,2,0,1:T(8,128)(2,1)}), bf16[2,8,96,1024]{3,2,0,1:T(8,128)(2,1)S(1)}, u32[]{:S(2)}, u32[]{:S(2)}) %all-to-all-start.1) | async-done | bytes 3145760 | tf_op jit(solution)/shard_map/all_to_all | solution.py:48
  396.3 3.4 bitcast_convert_fusion
  399.7 9.3 %gather_fusion.1 = f32[1024,1024]{1,0:T(8,128)} fusion(f32[1536,1024]{1,0:T(8,128)} %bitcast.90, s32[1024]{0:T(1024)S(1)} %broadcast_clamp_fusion), kind=kCustom, calls=%fused_computation.1 | custom fusion | bytes 8392704 | tf_op jit(solution)/shard_map/gather | solution.py:51
  409.0 4.2 fusion.10
  (46 shorter events, 2.4 us)
Async XLA Ops:
  6.5 143.0 %all-gather.5.cloned.1.call-start = ((), (), s32[]{:S(2)}) async-start(), calls=%async_computation.4 | async-start | bytes 7864320 | tf_op jit(solution)/shard_map/all_gather | solution.py:38
  104.0 93.5 %all-gather.7.cloned.1.call-start = ((), (), s32[]{:S(2)}) async-start(), calls=%async_computation.5 | async-start | bytes 7864320 | tf_op jit(solution)/shard_map/all_gather | solution.py:38
  104.7 211.4 %reduce-scatter.2.cloned.1.call-start = ((), (), s32[]{:S(2)}) async-start(), calls=%async_computation.3 | async-start | bytes 15728640 | tf_op jit(solution)/shard_map/reduce_scatter | solution.py:45
  149.5 6.6 %copy-start.1 = (bf16[1,1,768,4096]{3,2,1,0:T(8,128)(2,1)S(1)}, bf16[1,1,768,4096]{3,2,1,0:T(8,128)(2,1)}, u32[]{:S(2)}) copy-start(bf16[1,1,768,4096]{3,2,1,0:T(8,128)(2,1)} %all-gather.5.cloned.1.call-done) | copy-start | bytes 18874372
  149.5 12.5 %slice-start.2 = ((s8[6291456]{0:T(1024)(128)(4,1)}), s8[4194304]{0:T(1024)(128)(4,1)S(1)}, s32[]{:S(2)}) async-start(s8[6291456]{0:T(1024)(128)(4,1)} %bitcast.100), calls=%async_computation.8 | async-start | bytes 8388608
  156.1 5.9 %slice-start.3 = ((s8[6291456]{0:T(1024)(128)(4,1)}), s8[2097152]{0:T(1024)(128)(4,1)S(1)}, s32[]{:S(2)}) async-start(s8[6291456]{0:T(1024)(128)(4,1)} %bitcast.100), calls=%async_computation.9 | async-start | bytes 4194304
  197.5 6.6 %copy-start.2 = (bf16[1,1,768,4096]{3,2,1,0:T(8,128)(2,1)S(1)}, bf16[1,1,768,4096]{3,2,1,0:T(8,128)(2,1)}, u32[]{:S(2)}) copy-start(bf16[1,1,768,4096]{3,2,1,0:T(8,128)(2,1)} %all-gather.7.cloned.1.call-done) | copy-start | bytes 18874372
  197.5 12.4 %slice-start.4 = ((s8[6291456]{0:T(1024)(128)(4,1)}), s8[4194304]{0:T(1024)(128)(4,1)S(1)}, s32[]{:S(2)}) async-start(s8[6291456]{0:T(1024)(128)(4,1)} %bitcast.102), calls=%async_computation.10 | async-start | bytes 8388608
  197.5 16.0 %slice-start = ((s8[6291456]{0:T(1024)(128)(4,1)}), s8[4194304]{0:T(1024)(128)(4,1)S(1)}, s32[]{:S(2)}) async-start(s8[6291456]{0:T(1024)(128)(4,1)} %bitcast.93), calls=%async_computation.6 | async-start | bytes 8388608
  204.1 5.8 %slice-start.5 = ((s8[6291456]{0:T(1024)(128)(4,1)}), s8[2097152]{0:T(1024)(128)(4,1)S(1)}, s32[]{:S(2)}) async-start(s8[6291456]{0:T(1024)(128)(4,1)} %bitcast.102), calls=%async_computation.11 | async-start | bytes 4194304
  204.1 9.4 %slice-start.1 = ((s8[6291456]{0:T(1024)(128)(4,1)}), s8[2097152]{0:T(1024)(128)(4,1)S(1)}, s32[]{:S(2)}) async-start(s8[6291456]{0:T(1024)(128)(4,1)} %bitcast.93), calls=%async_computation.7 | async-start | bytes 4194304
  320.1 5.6 %copy-start = (f32[128,8]{0,1:T(8,128)S(1)}, f32[128,8]{0,1:T(8,128)}, u32[]{:S(2)}) copy-start(f32[128,8]{0,1:T(8,128)} %param.8) | copy-start | bytes 12292
  320.1 76.2 %all-to-all-start.1 = ((bf16[2,8,96,1024]{3,2,0,1:T(8,128)(2,1)}), bf16[2,8,96,1024]{3,2,0,1:T(8,128)(2,1)S(1)}, u32[]{:S(2)}, u32[]{:S(2)}) async-start(bf16[2,8,96,1024]{3,2,0,1:T(8,128)(2,1)} %copy.24), calls=%async_computation.2 | async-start | bytes 6291456 | tf_op jit(solution)/shard_map/all_to_all | solution.py:48
Sparse Core Ops, SparseCore 0:
  104.1 45.3 all-gather.4
  151.1 46.3 all-gather.6
  219.0 97.1 reduce-scatter.1
where the time goes:
time: 420 us
  waiting for transfers between devices  243 us (58%)
  blocking collectives  77.8 us (19%)
  matrix products  33.8 us (8%)
  local copies, waits for them, and re-layouts  27.5 us (7%)
  other arithmetic  18.3 us (4%)
  between operations  13.3 us (3%)
  starting transfers between devices  5.9 us (1%)
    reduce_scatter x1, waiting for transfers between devices, body(): lax.psum_scatter(partial_all.astype(jnp.bfloat16), 'etp', scatter_dimensi...  97.3 us
    all_to_all x1, blocking collectives, body(): lax.all_to_all(outgoing, 'ep', split_axis=0, concat_axis=2, tiled=True)  77.8 us
    all_gather x2, waiting for transfers between devices, body(): lax.all_gather(expert_rows, 'etp', axis=1, tiled=True)  74.6 us
    all_to_all x1, waiting for transfers between devices, body(): lax.all_to_all(summed.astype(jnp.bfloat16), 'ep', split_axis=1, concat_ax...  70.4 us
    dot_general x2, matrix products, add_features(): jnp.dot(portion, w_gate, preferred_element_type=jnp.float32)  13.1 us
    dot_general x2, matrix products, add_features(): jnp.dot(portion, w_up, preferred_element_type=jnp.float32)  11.6 us
    gather x1, local copies, waits for them, and re-layouts, body(): returned.reshape(experts * capacity, -1)[slot_index]  9.27 us
    dot_general x2, matrix products, body(): jnp.dot(hidden, down_weight[member], preferred_element_type=jnp.float32)  9 us
  transfers between devices with their start and end apart: 4, of which 4 were waited for; matrix products, arithmetic and copies ran while one was open for 4% of the time, Pallas kernels for 0%

commit v1 on v0

--- a/solution.py
+++ b/solution.py
@@ -35,7 +35,7 @@
         folder = partial(add_features, w_gate=gate_weight[member], w_up=up_weight[member])
         gate_sum, up_sum = folder(
             (starting, starting),
-            lax.all_gather(expert_rows, "etp", axis=1, tiled=True),
+            jnp.concatenate(lax.all_gather(expert_rows, "etp"), axis=1),
             jnp.int32(0),
         )
         hidden = (jax.nn.silu(gate_sum) * up_sum).astype(jnp.bfloat16)

time: 420 us -> 438 us (1.043)
  local copies, waits for them, and re-layouts: 27.5 us -> 44.9 us
    all_gather x0 -> x2, local copies, waits for them, and re-layouts: none -> 17.4 us  [body(): lax.all_gather(expert_rows, 'etp')]
where the time goes in v1:
time: 438 us
  waiting for transfers between devices  243 us (55%)
  blocking collectives  77.8 us (18%)
  local copies, waits for them, and re-layouts  44.9 us (10%)
  matrix products  34.6 us (8%)
  other arithmetic  18.3 us (4%)
  between operations  13.3 us (3%)
  starting transfers between devices  5.91 us (1%)
    reduce_scatter x1, waiting for transfers between devices, body(): lax.psum_scatter(partial_all.astype(jnp.bfloat16), 'etp', scatter_dimensi...  97.3 us
    all_to_all x1, blocking collectives, body(): lax.all_to_all(outgoing, 'ep', split_axis=0, concat_axis=2, tiled=True)  77.8 us
    all_gather x2, waiting for transfers between devices, body(): lax.all_gather(expert_rows, 'etp')  74.2 us
    all_to_all x1, waiting for transfers between devices, body(): lax.all_to_all(summed.astype(jnp.bfloat16), 'ep', split_axis=1, concat_ax...  70.4 us
    all_gather x2, local copies, waits for them, and re-layouts, body(): lax.all_gather(expert_rows, 'etp')  17.4 us
    dot_general x2, matrix products, add_features(): jnp.dot(portion, w_gate, preferred_element_type=jnp.float32)  16.3 us
    dot_general x2, matrix products, add_features(): jnp.dot(portion, w_up, preferred_element_type=jnp.float32)  11.1 us
    gather x1, local copies, waits for them, and re-layouts, body(): returned.reshape(experts * capacity, -1)[slot_index]  9.22 us
  transfers between devices with their start and end apart: 4, of which 4 were waited for; matrix products, arithmetic and copies ran while one was open for 4% of the time, Pallas kernels for 0%

profile of v1, /device:TPU:0, one launch (start us, length us, event | category | flops | bytes accessed | tf_op | source)
XLA Modules:
  0.0 437.6 jit_solution(13424729478029715407)
XLA Ops:
  8.2 4.5 %reduce-window.6 = s32[16,8,128]{2,1,0:T(8,128)S(1)} reduce-window(s32[16,8,128]{2,1,0:T(8,128)S(1)} %fusion.34, s32[]{:T(128)} %constant.32.clone.1), window={size=1x1x128 pad=0_0x0_0x127_0}, to_apply=%region_0.0 | reduce-window | flops 2080768 | bytes 131076 | tf_op jit(solution)/shard_map/reduce-window
  13.4 4.3 scatter_custom_fusion
  17.7 1.0 concatenate.5
  18.7 5.1 %gather_fusion = bf16[1536,1024]{1,0:T(8,128)(2,1)S(1)} fusion(bf16[129,1024]{1,0:T(8,128)(2,1)S(1)} %concatenate.5, s32[2048]{0:T(1024)S(1)} %pad_clamp_fusion), kind=kCustom, calls=%fused_computation | custom fusion | bytes 6297600 | tf_op jit(solution)/shard_map/gather | solution.py:29
  23.8 77.8 %all_to_all.27 = bf16[8,2,96,1024]{3,2,1,0:T(8,128)(2,1)S(1)} all-to-all(bf16[8,2,96,1024]{3,2,1,0:T(8,128)(2,1)S(1)} %bitcast.88), channel_id=1, replica_groups=mesh['ep'=8,'etp'=4] {'ep'}, dimensions={0} | all-to-all | bytes 6291456 | tf_op jit(solution)/shard_map/all_to_all | solution.py:30
  102.0 1.9 fusion.40
  105.0 44.6 %all-gather.5.cloned.1.call-done = bf16[4,1,768,1024]{3,2,1,0:T(8,128)(2,1)} async-done(((bf16[1,1,768,1024]{3,2,1,0:T(8,128)(2,1)}), bf16[4,1,768,1024]{3,2,1,0:T(8,128)(2,1)}) %all-gather.5.cloned.1.call-update) | async-done | bytes 6291472 | tf_op jit(solution)/shard_map/all_gather | solution.py:38
  149.5 8.7 %copy.26 = bf16[4,1,768,1024]{2,3,0,1:T(8,128)(2,1)} copy(bf16[4,1,768,1024]{3,2,1,0:T(8,128)(2,1)} %all-gather.5.cloned.1.call-done) | data formatting | bytes 12582912 | tf_op jit(solution)/shard_map/all_gather | solution.py:38
  158.2 9.6 %fusion.11 = f32[768,384]{1,0:T(8,128)} fusion(bf16[768,4096]{0,1:T(8,128)(2,1)} %bitcast.89, bf16[2,4096,384]{2,1,0:T(8,128)(2,1)} %param.9), kind=kOutput, calls=%fused_computation.19 | convolution fusion | flops 2415919104 | bytes 10616832 | tf_op jit(solution)/shard_map/dot_general | solution.py:10
  167.9 29.6 %all-gather.7.cloned.1.call-done = bf16[4,1,768,1024]{3,2,1,0:T(8,128)(2,1)} async-done(((bf16[1,1,768,1024]{3,2,1,0:T(8,128)(2,1)}), bf16[4,1,768,1024]{3,2,1,0:T(8,128)(2,1)}) %all-gather.7.cloned.1.call-update) | async-done | bytes 6291472 | tf_op jit(solution)/shard_map/all_gather | solution.py:38
  197.5 8.7 %copy.27 = bf16[4,1,768,1024]{2,3,0,1:T(8,128)(2,1)} copy(bf16[4,1,768,1024]{3,2,1,0:T(8,128)(2,1)} %all-gather.7.cloned.1.call-done) | data formatting | bytes 12582912 | tf_op jit(solution)/shard_map/all_gather | solution.py:38
  206.2 6.6 %fusion.6 = f32[768,384]{1,0:T(8,128)S(1)} fusion(bf16[768,4096]{0,1:T(8,128)(2,1)} %bitcast.93, bf16[2,4096,384]{2,1,0:T(8,128)(2,1)} %param.9), kind=kOutput, calls=%fused_computation.14 | convolution fusion | flops 2415919104 | bytes 10616832 | tf_op jit(solution)/shard_map/dot_general | solution.py:10
  212.9 5.5 %fusion.28 = bf16[768,384]{1,0:T(8,128)(2,1)S(1)} fusion(bf16[768,4096]{0,1:T(8,128)(2,1)S(1)} %bitcast.92, bf16[2,4096,384]{2,1,0:T(8,128)(2,1)} %param.10, f32[768,384]{1,0:T(8,128)S(1)} %copy-done.2), kind=kOutput, calls=%fused_computation.30 | convolution fusion | flops 2417688576 | bytes 11206656 | tf_op jit(solution)/shard_map/dot_general | solution.py:11
  218.5 5.5 %fusion.25 = bf16[768,384]{1,0:T(8,128)(2,1)S(1)} fusion(bf16[768,4096]{0,1:T(8,128)(2,1)S(1)} %bitcast.94, bf16[2,4096,384]{2,1,0:T(8,128)(2,1)} %param.10, f32[768,384]{1,0:T(8,128)S(1)} %fusion.6), kind=kOutput, calls=%fused_computation.29 | convolution fusion | flops 2417688576 | bytes 11206656 | tf_op jit(solution)/shard_map/dot_general | solution.py:11
  224.0 3.7 fusion
  227.7 3.7 fusion.1
  231.4 5.4 %pad_maximum_fusion = bf16[2,8,96,4096]{3,2,1,0:T(8,128)(2,1)} fusion(bf16[1,8,96,4096]{3,2,1,0:T(8,128)(2,1)S(1)} %fusion.1, bf16[1,8,96,4096]{3,2,1,0:T(8,128)(2,1)S(1)} %fusion), kind=kLoop, calls=%fused_computation.3 | loop fusion | flops 6291456 | bytes 25165824 | tf_op jit(solution)/shard_map/stack | solution.py:43
  236.8 97.3 %reduce-scatter.2.cloned.1.call-done = bf16[2,8,96,1024]{3,2,1,0:T(8,128)(2,1)} async-done(((bf16[2,8,96,4096]{3,2,1,0:T(8,128)(2,1)}), bf16[2,8,96,1024]{3,2,1,0:T(8,128)(2,1)}) %reduce-scatter.2.cloned.1.call-update) | async-done | bytes 3145744 | tf_op jit(solution)/shard_map/reduce_scatter | solution.py:45
  334.1 4.0 copy.28
  338.0 5.7 %all-to-all-start.1 = ((bf16[2,8,96,1024]{3,2,0,1:T(8,128)(2,1)}), bf16[2,8,96,1024]{3,2,0,1:T(8,128)(2,1)S(1)}, u32[]{:S(2)}, u32[]{:S(2)}) async-start(bf16[2,8,96,1024]{3,2,0,1:T(8,128)(2,1)} %copy.28), calls=%async_computation.2 | async-start | bytes 6291456 | tf_op jit(solution)/shard_map/all_to_all | solution.py:48
  343.8 70.4 %all-to-all-done.1 = bf16[2,8,96,1024]{3,2,0,1:T(8,128)(2,1)S(1)} async-done(((bf16[2,8,96,1024]{3,2,0,1:T(8,128)(2,1)}), bf16[2,8,96,1024]{3,2,0,1:T(8,128)(2,1)S(1)}, u32[]{:S(2)}, u32[]{:S(2)}) %all-to-all-start.1) | async-done | bytes 3145760 | tf_op jit(solution)/shard_map/all_to_all | solution.py:48
  414.2 3.4 bitcast_convert_fusion
  417.6 9.2 %gather_fusion.1 = f32[1024,1024]{1,0:T(8,128)} fusion(f32[1536,1024]{1,0:T(8,128)} %bitcast.86, s32[1024]{0:T(1024)S(1)} %broadcast_clamp_fusion), kind=kCustom, calls=%fused_computation.1 | custom fusion | bytes 8392704 | tf_op jit(solution)/shard_map/gather | solution.py:51
  426.9 4.2 fusion.2
  (43 shorter events, 3.9 us)
Async XLA Ops:
  6.5 143.0 %all-gather.5.cloned.1.call-start = ((), (), s32[]{:S(2)}) async-start(), calls=%async_computation.4 | async-start | bytes 7864320 | tf_op jit(solution)/shard_map/all_gather | solution.py:38
  104.0 93.5 %all-gather.7.cloned.1.call-start = ((), (), s32[]{:S(2)}) async-start(), calls=%async_computation.5 | async-start | bytes 7864320 | tf_op jit(solution)/shard_map/all_gather | solution.py:38
  104.7 229.4 %reduce-scatter.2.cloned.1.call-start = ((), (), s32[]{:S(2)}) async-start(), calls=%async_computation.3 | async-start | bytes 15728640 | tf_op jit(solution)/shard_map/reduce_scatter | solution.py:45
  197.5 15.4 %slice-start = ((s8[6291456]{0:T(1024)(128)(4,1)}), s8[2097152]{0:T(1024)(128)(4,1)S(1)}, s32[]{:S(2)}) async-start(s8[6291456]{0:T(1024)(128)(4,1)} %bitcast.90), calls=%async_computation.6 | async-start | bytes 4194304
  206.2 6.6 %slice-start.1 = ((s8[6291456]{0:T(1024)(128)(4,1)}), s8[4194304]{0:T(1024)(128)(4,1)S(1)}, s32[]{:S(2)}) async-start(s8[6291456]{0:T(1024)(128)(4,1)} %bitcast.90), calls=%async_computation.7 | async-start | bytes 8388608
  206.2 6.7 %copy-start.2 = (f32[768,384]{1,0:T(8,128)S(1)}, f32[768,384]{1,0:T(8,128)}, u32[]{:S(2)}) copy-start(f32[768,384]{1,0:T(8,128)} %fusion.11) | copy-start | bytes 3538948
  212.9 5.6 %copy-start = (bf16[4,1,768,1024]{2,3,0,1:T(8,128)(2,1)S(1)}, bf16[4,1,768,1024]{2,3,0,1:T(8,128)(2,1)}, u32[]{:S(2)}) copy-start(bf16[4,1,768,1024]{2,3,0,1:T(8,128)(2,1)} %copy.27) | copy-start | bytes 18874372
  212.9 11.1 %slice-start.2 = ((s8[6291456]{0:T(1024)(128)(4,1)}), s8[4194304]{0:T(1024)(128)(4,1)S(1)}, s32[]{:S(2)}) async-start(s8[6291456]{0:T(1024)(128)(4,1)} %bitcast.100), calls=%async_computation.8 | async-start | bytes 8388608
  218.4 5.6 %slice-start.3 = ((s8[6291456]{0:T(1024)(128)(4,1)}), s8[2097152]{0:T(1024)(128)(4,1)S(1)}, s32[]{:S(2)}) async-start(s8[6291456]{0:T(1024)(128)(4,1)} %bitcast.100), calls=%async_computation.9 | async-start | bytes 4194304
  338.0 5.7 %copy-start.1 = (f32[128,8]{0,1:T(8,128)S(1)}, f32[128,8]{0,1:T(8,128)}, u32[]{:S(2)}) copy-start(f32[128,8]{0,1:T(8,128)} %param.8) | copy-start | bytes 12292
  338.0 76.2 %all-to-all-start.1 = ((bf16[2,8,96,1024]{3,2,0,1:T(8,128)(2,1)}), bf16[2,8,96,1024]{3,2,0,1:T(8,128)(2,1)S(1)}, u32[]{:S(2)}, u32[]{:S(2)}) async-start(bf16[2,8,96,1024]{3,2,0,1:T(8,128)(2,1)} %copy.28), calls=%async_computation.2 | async-start | bytes 6291456 | tf_op jit(solution)/shard_map/all_to_all | solution.py:48
Sparse Core Ops, SparseCore 0:
  104.1 45.3 all-gather.4
  151.1 46.3 all-gather.6
  236.9 97.1 reduce-scatter.1
